TPU v7x, 512 devices: a whole 4x8x8 slice. The times are simulated.
512 devices in a mesh: rows: 128 (over x_hi, z, y), feat: 4 (over x_lo, core).
Axes of the slice: x: 4 (x_hi: 2, x_lo: 2; x = x_hi * 2 + x_lo), y: 8, z: 8, core: 2. Of those that a mesh axis runs over, the one named last changes fastest.
Arguments:
- features: bfloat16 [131072, 64], P('rows', 'feat'), may hold values from -0.75 to 0.75
- probes: bfloat16 [131072, 32], P('rows', 'feat'), may hold values from -6 to 6
- theta: float32 [1], replicated, may hold values from 0.18 to 0.69
- block_mask: int32 [128, 9], P('rows'), may hold values 0 or 1
- order: int32 [128, 1024], P('rows'), may hold values from 0 to 1023, each once within a row
Outputs:
- kernel_probes: float32 [131072, 32], P('rows', 'feat')
- deriv_probes: float32 [131072, 32], P('rows', 'feat')
All inputs are finite; a program needn't handle non-finite values. No bound on the sum of `block_mask` on one device may be relied on, other than what follows from the above.
Results may differ from a plain program's by a relative error of at most 0.003.
Values may be sent and summed in bfloat16 or wider, within the bound.
A program may use at most 64 MiB of HBM per device.

v0:
```python
import jax
import jax.numpy as jnp
from jax import lax
from jax.sharding import PartitionSpec as P


def sent_to_all(value, axis):
    copies = jnp.broadcast_to(value, (lax.axis_size(axis), *value.shape))
    return lax.all_to_all(copies, axis, split_axis=0, concat_axis=0, tiled=True)


def in_order(tiles, dim):
    shape = list(tiles.shape[1:])
    shape[dim] *= tiles.shape[0]
    return jnp.moveaxis(tiles, 0, dim).reshape(shape)


def collect(value, axis, dim):
    tiles = sent_to_all(value, axis)
    return in_order(tiles, dim)


def passed_along(value, axis, steps):
    count = lax.axis_size(axis)
    pairs = [(source, (source + steps) % count) for source in range(count)]
    return lax.ppermute(value, axis, pairs)


def split_up(value, dim, devices):
    shape = value.shape
    tiles = value.reshape(*shape[:dim], devices, shape[dim] // devices, *shape[dim + 1 :])
    return jnp.moveaxis(tiles, dim, 0)


def sent_and_summed(value, axis, dim):
    tiles = split_up(value, dim, lax.axis_size(axis))
    arrived = lax.all_to_all(tiles, axis, split_axis=0, concat_axis=0, tiled=True)
    return arrived.sum(axis=0)


def sent_together(arrays, axis, dim, along):
    widths = [a.shape[along] for a in arrays]
    both = jnp.concatenate(arrays, axis=along)
    out = sent_and_summed(both, axis, dim)
    return tuple(jnp.split(out, [sum(widths[:k]) for k in range(1, len(widths))], axis=along))


def body(features, probes, theta, block_mask, order):
    own_full = lax.all_gather(features, "feat", axis=1, tiled=True)
    scale = jnp.exp(-2.0 * theta[0])
    own_sq = jnp.sum(own_full.astype(jnp.float32) ** 2, axis=1)
    rows_here = probes.shape[0]

    def tile_terms(panel_full, panel_probes, active):
        panel_sq = jnp.sum(panel_full.astype(jnp.float32) ** 2, axis=1)
        cross = lax.dot_general(
            own_full, panel_full, (((1,), (1,)), ((), ())), preferred_element_type=jnp.float32
        )
        dist2 = jnp.maximum(own_sq[:, None] + panel_sq[None, :] - 2.0 * cross, 0.0)
        radius2 = dist2 * scale
        radius = jnp.sqrt(radius2)
        inside = jnp.maximum(1.0 - radius, 0.0)
        inside2 = inside * inside
        kern = (inside2 * inside2 * (4.0 * radius + 1.0)).astype(jnp.bfloat16)
        deriv = (20.0 * radius2 * inside2 * inside).astype(jnp.bfloat16)
        first = jnp.dot(kern, panel_probes, preferred_element_type=jnp.float32)
        second = jnp.dot(deriv, panel_probes, preferred_element_type=jnp.float32)
        weight = (active > 0).astype(jnp.float32)
        return (first * weight, second * weight)

    all_probes = collect(probes, "feat", 1)
    ordered_all = jnp.take(all_probes, order[0], axis=0)
    quarter = rows_here // lax.axis_size("feat")
    start = lax.axis_index("feat") * quarter
    carried = lax.dynamic_slice_in_dim(own_full, start, quarter, 0)
    panel_probes = lax.dynamic_slice_in_dim(ordered_all, start, quarter, 0)
    total_k, total_d = tile_terms(carried, panel_probes, jnp.int32(1))
    upper = (carried, panel_probes)
    lower = (carried, panel_probes)
    for step in range(1, 5):
        upper = passed_along((upper[0], upper[1]), "rows", -1)
        lower = passed_along((lower[0], lower[1]), "rows", 1)
        add_k, add_d = tile_terms(upper[0], upper[1], block_mask[0, 4 + step])
        total_k, total_d = (total_k + add_k, total_d + add_d)
        add_k, add_d = tile_terms(lower[0], lower[1], block_mask[0, 4 - step])
        total_k, total_d = (total_k + add_k, total_d + add_d)
    total_k, total_d = sent_together((total_k, total_d), "feat", 1, 0)
    return (total_k, total_d)


def solution(mesh):
    return jax.shard_map(
        body,
        mesh=mesh,
        in_specs=(P("rows", "feat"), P("rows", "feat"), P(), P("rows", None), P("rows", None)),
        out_specs=(P("rows", "feat"), P("rows", "feat")),
        check_vma=False,
    )
```

profile of v0, /device:TPU:1, one launch (start us, length us, event | category | flops | bytes accessed | tf_op | source)
XLA Modules:
  0.0 137.9 jit_solution(5949143357094899956)
XLA Ops:
  0.6 12.3 %all_gather.3 = bf16[1024,64]{0,1:T(8,128)(2,1)S(1)} all-gather(bf16[1024,16]{0,1:T(8,128)(2,1)} %param.5), channel_id=1, replica_groups=mesh['rows'=128,'feat'=4] {'feat'}, dimensions={1}, use_global_device_ids=true | all-gather | bytes 163840 | tf_op jit(solution)/shard_map/all_gather | solution.py:49
  13.0 10.7 %collective-permute-start = (bf16[256,64]{0,1:T(8,128)(2,1)S(1)}, bf16[256,64]{0,1:T(8,128)(2,1)S(1)}, u32[]{:S(2)}, u32[]{:S(2)}) collective-permute-start(bf16[256,64]{0,1:T(8,128)(2,1)S(1)} %get-tuple-element.3), channel_id=1, source_target_pairs={{0,508},{4,0},{8,4},{12,8},{16,12},{20,16},{24,20},{28,24},{32,28}... | collective-permute-start | bytes 98312 | tf_op jit(solution)/shard_map/ppermute | solution.py:26
  23.7 1.9 %collective-permute-start.2 = (bf16[256,64]{0,1:T(8,128)(2,1)S(1)}, bf16[256,64]{0,1:T(8,128)(2,1)S(1)}, u32[]{:S(2)}, u32[]{:S(2)}) collective-permute-start(bf16[256,64]{0,1:T(8,128)(2,1)S(1)} %get-tuple-element.3), channel_id=1, source_target_pairs={{0,4},{4,8},{8,12},{12,16},{16,20},{20,24},{24,28},{28,32},{32,36}... | collective-permute-start | bytes 98312 | tf_op jit(solution)/shard_map/ppermute | solution.py:26
  25.6 0.6 broadcast_in_dim.13
  26.2 3.7 %all-to-all-start = ((bf16[4,1024,8]{1,2,0:T(8,128)(2,1)}), bf16[4,1024,8]{1,2,0:T(8,128)(2,1)S(1)}, u32[]{:S(2)}, u32[]{:S(2)}) async-start(bf16[4,1024,8]{1,2,0:T(8,128)(2,1)} %broadcast_in_dim.13), calls=%async_computation | async-start | bytes 131072 | tf_op jit(solution)/shard_map/all_to_all | solution.py:9
  30.0 0.0 copy-start.2
  30.7 0.0 copy-start
  30.7 1.3 fusion.11
  32.1 0.7 fusion.85
  32.8 0.1 dynamic-slice
  37.9 0.0 collective-permute-done
  37.9 9.4 %collective-permute-start.4 = (bf16[256,64]{0,1:T(8,128)(2,1)S(1)}, bf16[256,64]{0,1:T(8,128)(2,1)S(1)}, u32[]{:S(2)}, u32[]{:S(2)}) collective-permute-start(bf16[256,64]{0,1:T(8,128)(2,1)S(1)} %collective-permute-done), channel_id=1, source_target_pairs={{0,508},{4,0},{8,4},{12,8},{16,12},{20,16},{24,20},{28,24},{32,28}... | collective-permute-start | bytes 98312 | tf_op jit(solution)/shard_map/ppermute | solution.py:26
  47.3 0.0 collective-permute-done.2
  47.3 1.9 %collective-permute-start.6 = (bf16[256,64]{0,1:T(8,128)(2,1)S(1)}, bf16[256,64]{0,1:T(8,128)(2,1)S(1)}, u32[]{:S(2)}, u32[]{:S(2)}) collective-permute-start(bf16[256,64]{0,1:T(8,128)(2,1)S(1)} %collective-permute-done.2), channel_id=1, source_target_pairs={{0,4},{4,8},{8,12},{12,16},{16,20},{20,24},{24,28},{28,32},{32,36}... | collective-permute-start | bytes 98312 | tf_op jit(solution)/shard_map/ppermute | solution.py:26
  49.2 0.3 fusion.6
  49.5 0.3 fusion.7
  49.9 0.0 all-to-all-done
  49.9 0.2 copy.8
  50.1 3.2 %gather_fusion = bf16[1024,32]{1,0:T(8,128)(2,1)S(1)} fusion(bf16[1024,32]{1,0:T(8,128)(2,1)S(1)} %copy.8, s32[1024]{0:T(1024)S(1)} %broadcast_clamp_fusion), kind=kCustom, calls=%fused_computation | custom fusion | bytes 135168 | tf_op jit(solution)/shard_map/jit(_take)/gather | solution.py:72
  53.3 0.1 dynamic-slice_select_fusion
  53.4 2.1 %collective-permute-start.3 = (bf16[256,32]{1,0:T(8,128)(2,1)S(1)}, bf16[256,32]{1,0:T(8,128)(2,1)S(1)}, u32[]{:S(2)}, u32[]{:S(2)}) collective-permute-start(bf16[256,32]{1,0:T(8,128)(2,1)S(1)} %dynamic-slice_select_fusion), channel_id=1, source_target_pairs={{0,4},{4,8},{8,12},{12,16},{16,20},{20,24},{24,28},{28,32},{32,36}... | collective-permute-start | bytes 49160 | tf_op jit(solution)/shard_map/ppermute | solution.py:26
  55.5 9.1 %collective-permute-start.1 = (bf16[256,32]{1,0:T(8,128)(2,1)S(1)}, bf16[256,32]{1,0:T(8,128)(2,1)S(1)}, u32[]{:S(2)}, u32[]{:S(2)}) collective-permute-start(bf16[256,32]{1,0:T(8,128)(2,1)S(1)} %dynamic-slice_select_fusion), channel_id=1, source_target_pairs={{0,508},{4,0},{8,4},{12,8},{16,12},{20,16},{24,20},{28,24},{32,28}... | collective-permute-start | bytes 49160 | tf_op jit(solution)/shard_map/ppermute | solution.py:26
  64.5 1.8 %fusion.28 = f32[1024,32]{0,1:T(8,128)S(1)} fusion(bf16[256,32]{1,0:T(8,128)(2,1)S(1)} %dynamic-slice_select_fusion, f32[1024,256]{0,1:T(8,128)} %fusion.11), kind=kOutput, calls=%fused_computation.89 | convolution fusion | flops 18612224 | bytes 1196032 | tf_op jit(solution)/shard_map/dot_general | solution.py:67
  66.4 0.6 fusion.29
  67.0 3.4 %collective-permute-start.8 = (bf16[256,64]{0,1:T(8,128)(2,1)S(1)}, bf16[256,64]{0,1:T(8,128)(2,1)S(1)}, u32[]{:S(2)}, u32[]{:S(2)}) collective-permute-start(bf16[256,64]{0,1:T(8,128)(2,1)S(1)} %collective-permute-done.4), channel_id=1, source_target_pairs={{0,508},{4,0},{8,4},{12,8},{16,12},{20,16},{24,20},{28,24},{32,28}... | collective-permute-start | bytes 98312 | tf_op jit(solution)/shard_map/ppermute | solution.py:26
  70.4 1.9 %collective-permute-start.10 = (bf16[256,64]{0,1:T(8,128)(2,1)S(1)}, bf16[256,64]{0,1:T(8,128)(2,1)S(1)}, u32[]{:S(2)}, u32[]{:S(2)}) collective-permute-start(bf16[256,64]{0,1:T(8,128)(2,1)S(1)} %collective-permute-done.6), channel_id=1, source_target_pairs={{0,4},{4,8},{8,12},{12,16},{16,20},{20,24},{24,28},{28,32},{32,36}... | collective-permute-start | bytes 98312 | tf_op jit(solution)/shard_map/ppermute | solution.py:26
  72.3 0.3 fusion.4
  72.7 0.3 fusion.5
  73.0 0.0 collective-permute-done.3
  73.0 1.9 %collective-permute-start.7 = (bf16[256,32]{1,0:T(8,128)(2,1)S(1)}, bf16[256,32]{1,0:T(8,128)(2,1)S(1)}, u32[]{:S(2)}, u32[]{:S(2)}) collective-permute-start(bf16[256,32]{1,0:T(8,128)(2,1)S(1)} %collective-permute-done.3), channel_id=1, source_target_pairs={{0,4},{4,8},{8,12},{12,16},{16,20},{20,24},{24,28},{28,32},{32,36}... | collective-permute-start | bytes 49160 | tf_op jit(solution)/shard_map/ppermute | solution.py:26
  74.9 9.1 %collective-permute-start.5 = (bf16[256,32]{1,0:T(8,128)(2,1)S(1)}, bf16[256,32]{1,0:T(8,128)(2,1)S(1)}, u32[]{:S(2)}, u32[]{:S(2)}) collective-permute-start(bf16[256,32]{1,0:T(8,128)(2,1)S(1)} %collective-permute-done.1), channel_id=1, source_target_pairs={{0,508},{4,0},{8,4},{12,8},{16,12},{20,16},{24,20},{28,24},{32,28}... | collective-permute-start | bytes 49160 | tf_op jit(solution)/shard_map/ppermute | solution.py:26
  84.0 0.8 fusion.19
  84.8 0.8 fusion.27
  85.7 0.8 fusion.26
  86.5 0.8 fusion.18
  87.3 1.9 %collective-permute-start.11 = (bf16[256,32]{1,0:T(8,128)(2,1)S(1)}, bf16[256,32]{1,0:T(8,128)(2,1)S(1)}, u32[]{:S(2)}, u32[]{:S(2)}) collective-permute-start(bf16[256,32]{1,0:T(8,128)(2,1)S(1)} %collective-permute-done.7), channel_id=1, source_target_pairs={{0,4},{4,8},{8,12},{12,16},{16,20},{20,24},{24,28},{28,32},{32,36}... | collective-permute-start | bytes 49160 | tf_op jit(solution)/shard_map/ppermute | solution.py:26
  89.3 0.8 convolution_multiply_fusion.13
  90.1 0.8 convolution_multiply_fusion.21
  90.9 0.0 collective-permute-done.5
  90.9 9.1 %collective-permute-start.9 = (bf16[256,32]{1,0:T(8,128)(2,1)S(1)}, bf16[256,32]{1,0:T(8,128)(2,1)S(1)}, u32[]{:S(2)}, u32[]{:S(2)}) collective-permute-start(bf16[256,32]{1,0:T(8,128)(2,1)S(1)} %collective-permute-done.5), channel_id=1, source_target_pairs={{0,508},{4,0},{8,4},{12,8},{16,12},{20,16},{24,20},{28,24},{32,28}... | collective-permute-start | bytes 49160 | tf_op jit(solution)/shard_map/ppermute | solution.py:26
  100.0 0.8 fusion.17
  100.8 0.8 fusion.25
  101.6 0.0 collective-permute-done.8
  101.7 1.9 %collective-permute-start.12 = (bf16[256,64]{0,1:T(8,128)(2,1)S(1)}, bf16[256,64]{0,1:T(8,128)(2,1)S(1)}, u32[]{:S(2)}, u32[]{:S(2)}) collective-permute-start(bf16[256,64]{0,1:T(8,128)(2,1)S(1)} %collective-permute-done.8), channel_id=1, source_target_pairs={{0,508},{4,0},{8,4},{12,8},{16,12},{20,16},{24,20},{28,24},{32,28}... | collective-permute-start | bytes 98312 | tf_op jit(solution)/shard_map/ppermute | solution.py:26
  103.6 3.4 %collective-permute-start.14 = (bf16[256,64]{0,1:T(8,128)(2,1)S(1)}, bf16[256,64]{0,1:T(8,128)(2,1)S(1)}, u32[]{:S(2)}, u32[]{:S(2)}) collective-permute-start(bf16[256,64]{0,1:T(8,128)(2,1)S(1)} %collective-permute-done.10), channel_id=1, source_target_pairs={{0,4},{4,8},{8,12},{12,16},{16,20},{20,24},{24,28},{28,32},{32,36}... | collective-permute-start | bytes 98312 | tf_op jit(solution)/shard_map/ppermute | solution.py:26
  107.0 0.3 fusion.2
  107.3 0.3 fusion.3
  107.7 0.0 collective-permute-done.11
  107.7 1.9 %collective-permute-start.15 = (bf16[256,32]{1,0:T(8,128)(2,1)S(1)}, bf16[256,32]{1,0:T(8,128)(2,1)S(1)}, u32[]{:S(2)}, u32[]{:S(2)}) collective-permute-start(bf16[256,32]{1,0:T(8,128)(2,1)S(1)} %collective-permute-done.11), channel_id=1, source_target_pairs={{0,4},{4,8},{8,12},{12,16},{16,20},{20,24},{24,28},{28,32},{32,36}... | collective-permute-start | bytes 49160 | tf_op jit(solution)/shard_map/ppermute | solution.py:26
  109.6 0.8 convolution_multiply_fusion.11
  110.4 0.8 convolution_multiply_fusion.19
  111.2 0.0 collective-permute-done.9
  111.2 9.3 %collective-permute-start.13 = (bf16[256,32]{1,0:T(8,128)(2,1)S(1)}, bf16[256,32]{1,0:T(8,128)(2,1)S(1)}, u32[]{:S(2)}, u32[]{:S(2)}) collective-permute-start(bf16[256,32]{1,0:T(8,128)(2,1)S(1)} %collective-permute-done.9), channel_id=1, source_target_pairs={{0,508},{4,0},{8,4},{12,8},{16,12},{20,16},{24,20},{28,24},{32,28}... | collective-permute-start | bytes 49160 | tf_op jit(solution)/shard_map/ppermute | solution.py:26
  120.5 0.8 fusion.23
  121.3 0.8 fusion.15
  122.2 0.3 fusion
  122.5 0.0 collective-permute-done.15
  122.5 0.8 convolution_multiply_fusion.9
  123.3 0.8 convolution_multiply_fusion.17
  124.2 0.3 fusion.1
  124.5 0.8 fusion.13
  125.3 0.8 fusion.21
  126.2 11.1 %all_to_all.10 = f32[4,2048,8]{1,2,0:T(8,128)S(1)} all-to-all(f32[4,2048,8]{1,2,0:T(8,128)S(1)} %maximum_bitcast_fusion), channel_id=1, replica_groups=mesh['rows'=128,'feat'=4] {'feat'}, dimensions={0} | all-to-all | bytes 524288 | tf_op jit(solution)/shard_map/all_to_all | solution.py:37
  137.3 0.6 fusion.84
  (29 shorter events, 0.4 us)
Async XLA Ops:
  12.9 12.7 %copy-start.1 = (bf16[1024,8]{0,1:T(8,128)(2,1)S(1)}, bf16[1024,8]{0,1:T(8,128)(2,1)}, u32[]{:S(2)}) copy-start(bf16[1024,8]{0,1:T(8,128)(2,1)} %param.6) | copy-start | bytes 49156
  13.0 24.9 %collective-permute-start = (bf16[256,64]{0,1:T(8,128)(2,1)S(1)}, bf16[256,64]{0,1:T(8,128)(2,1)S(1)}, u32[]{:S(2)}, u32[]{:S(2)}) collective-permute-start(bf16[256,64]{0,1:T(8,128)(2,1)S(1)} %get-tuple-element.3), channel_id=1, source_target_pairs={{0,508},{4,0},{8,4},{12,8},{16,12},{20,16},{24,20},{28,24},{32,28}... | collective-permute-start | bytes 98312 | tf_op jit(solution)/shard_map/ppermute | solution.py:26
  23.7 23.6 %collective-permute-start.2 = (bf16[256,64]{0,1:T(8,128)(2,1)S(1)}, bf16[256,64]{0,1:T(8,128)(2,1)S(1)}, u32[]{:S(2)}, u32[]{:S(2)}) collective-permute-start(bf16[256,64]{0,1:T(8,128)(2,1)S(1)} %get-tuple-element.3), channel_id=1, source_target_pairs={{0,4},{4,8},{8,12},{12,16},{16,20},{20,24},{24,28},{28,32},{32,36}... | collective-permute-start | bytes 98312 | tf_op jit(solution)/shard_map/ppermute | solution.py:26
  26.2 23.6 %all-to-all-start = ((bf16[4,1024,8]{1,2,0:T(8,128)(2,1)}), bf16[4,1024,8]{1,2,0:T(8,128)(2,1)S(1)}, u32[]{:S(2)}, u32[]{:S(2)}) async-start(bf16[4,1024,8]{1,2,0:T(8,128)(2,1)} %broadcast_in_dim.13), calls=%async_computation | async-start | bytes 131072 | tf_op jit(solution)/shard_map/all_to_all | solution.py:9
  30.0 0.7 copy-start.2
  30.7 1.4 copy-start
  37.9 29.1 %collective-permute-start.4 = (bf16[256,64]{0,1:T(8,128)(2,1)S(1)}, bf16[256,64]{0,1:T(8,128)(2,1)S(1)}, u32[]{:S(2)}, u32[]{:S(2)}) collective-permute-start(bf16[256,64]{0,1:T(8,128)(2,1)S(1)} %collective-permute-done), channel_id=1, source_target_pairs={{0,508},{4,0},{8,4},{12,8},{16,12},{20,16},{24,20},{28,24},{32,28}... | collective-permute-start | bytes 98312 | tf_op jit(solution)/shard_map/ppermute | solution.py:26
  47.3 23.1 %collective-permute-start.6 = (bf16[256,64]{0,1:T(8,128)(2,1)S(1)}, bf16[256,64]{0,1:T(8,128)(2,1)S(1)}, u32[]{:S(2)}, u32[]{:S(2)}) collective-permute-start(bf16[256,64]{0,1:T(8,128)(2,1)S(1)} %collective-permute-done.2), channel_id=1, source_target_pairs={{0,4},{4,8},{8,12},{12,16},{16,20},{20,24},{24,28},{28,32},{32,36}... | collective-permute-start | bytes 98312 | tf_op jit(solution)/shard_map/ppermute | solution.py:26
  53.3 13.1 %copy-start.3 = (f32[1024,256]{0,1:T(8,128)S(1)}, f32[1024,256]{0,1:T(8,128)}, u32[]{:S(2)}) copy-start(f32[1024,256]{0,1:T(8,128)} %fusion.11) | copy-start | bytes 3145732
  53.4 19.6 %collective-permute-start.3 = (bf16[256,32]{1,0:T(8,128)(2,1)S(1)}, bf16[256,32]{1,0:T(8,128)(2,1)S(1)}, u32[]{:S(2)}, u32[]{:S(2)}) collective-permute-start(bf16[256,32]{1,0:T(8,128)(2,1)S(1)} %dynamic-slice_select_fusion), channel_id=1, source_target_pairs={{0,4},{4,8},{8,12},{12,16},{16,20},{20,24},{24,28},{28,32},{32,36}... | collective-permute-start | bytes 49160 | tf_op jit(solution)/shard_map/ppermute | solution.py:26
  55.5 19.5 %collective-permute-start.1 = (bf16[256,32]{1,0:T(8,128)(2,1)S(1)}, bf16[256,32]{1,0:T(8,128)(2,1)S(1)}, u32[]{:S(2)}, u32[]{:S(2)}) collective-permute-start(bf16[256,32]{1,0:T(8,128)(2,1)S(1)} %dynamic-slice_select_fusion), channel_id=1, source_target_pairs={{0,508},{4,0},{8,4},{12,8},{16,12},{20,16},{24,20},{28,24},{32,28}... | collective-permute-start | bytes 49160 | tf_op jit(solution)/shard_map/ppermute | solution.py:26
  67.0 34.6 %collective-permute-start.8 = (bf16[256,64]{0,1:T(8,128)(2,1)S(1)}, bf16[256,64]{0,1:T(8,128)(2,1)S(1)}, u32[]{:S(2)}, u32[]{:S(2)}) collective-permute-start(bf16[256,64]{0,1:T(8,128)(2,1)S(1)} %collective-permute-done.4), channel_id=1, source_target_pairs={{0,508},{4,0},{8,4},{12,8},{16,12},{20,16},{24,20},{28,24},{32,28}... | collective-permute-start | bytes 98312 | tf_op jit(solution)/shard_map/ppermute | solution.py:26
  70.4 33.2 %collective-permute-start.10 = (bf16[256,64]{0,1:T(8,128)(2,1)S(1)}, bf16[256,64]{0,1:T(8,128)(2,1)S(1)}, u32[]{:S(2)}, u32[]{:S(2)}) collective-permute-start(bf16[256,64]{0,1:T(8,128)(2,1)S(1)} %collective-permute-done.6), channel_id=1, source_target_pairs={{0,4},{4,8},{8,12},{12,16},{16,20},{20,24},{24,28},{28,32},{32,36}... | collective-permute-start | bytes 98312 | tf_op jit(solution)/shard_map/ppermute | solution.py:26
  73.0 14.3 %collective-permute-start.7 = (bf16[256,32]{1,0:T(8,128)(2,1)S(1)}, bf16[256,32]{1,0:T(8,128)(2,1)S(1)}, u32[]{:S(2)}, u32[]{:S(2)}) collective-permute-start(bf16[256,32]{1,0:T(8,128)(2,1)S(1)} %collective-permute-done.3), channel_id=1, source_target_pairs={{0,4},{4,8},{8,12},{12,16},{16,20},{20,24},{24,28},{28,32},{32,36}... | collective-permute-start | bytes 49160 | tf_op jit(solution)/shard_map/ppermute | solution.py:26
  74.9 16.0 %collective-permute-start.5 = (bf16[256,32]{1,0:T(8,128)(2,1)S(1)}, bf16[256,32]{1,0:T(8,128)(2,1)S(1)}, u32[]{:S(2)}, u32[]{:S(2)}) collective-permute-start(bf16[256,32]{1,0:T(8,128)(2,1)S(1)} %collective-permute-done.1), channel_id=1, source_target_pairs={{0,508},{4,0},{8,4},{12,8},{16,12},{20,16},{24,20},{28,24},{32,28}... | collective-permute-start | bytes 49160 | tf_op jit(solution)/shard_map/ppermute | solution.py:26
  87.3 20.3 %collective-permute-start.11 = (bf16[256,32]{1,0:T(8,128)(2,1)S(1)}, bf16[256,32]{1,0:T(8,128)(2,1)S(1)}, u32[]{:S(2)}, u32[]{:S(2)}) collective-permute-start(bf16[256,32]{1,0:T(8,128)(2,1)S(1)} %collective-permute-done.7), channel_id=1, source_target_pairs={{0,4},{4,8},{8,12},{12,16},{16,20},{20,24},{24,28},{28,32},{32,36}... | collective-permute-start | bytes 49160 | tf_op jit(solution)/shard_map/ppermute | solution.py:26
  90.9 20.3 %collective-permute-start.9 = (bf16[256,32]{1,0:T(8,128)(2,1)S(1)}, bf16[256,32]{1,0:T(8,128)(2,1)S(1)}, u32[]{:S(2)}, u32[]{:S(2)}) collective-permute-start(bf16[256,32]{1,0:T(8,128)(2,1)S(1)} %collective-permute-done.5), channel_id=1, source_target_pairs={{0,508},{4,0},{8,4},{12,8},{16,12},{20,16},{24,20},{28,24},{32,28}... | collective-permute-start | bytes 49160 | tf_op jit(solution)/shard_map/ppermute | solution.py:26
  101.7 22.5 %collective-permute-start.12 = (bf16[256,64]{0,1:T(8,128)(2,1)S(1)}, bf16[256,64]{0,1:T(8,128)(2,1)S(1)}, u32[]{:S(2)}, u32[]{:S(2)}) collective-permute-start(bf16[256,64]{0,1:T(8,128)(2,1)S(1)} %collective-permute-done.8), channel_id=1, source_target_pairs={{0,508},{4,0},{8,4},{12,8},{16,12},{20,16},{24,20},{28,24},{32,28}... | collective-permute-start | bytes 98312 | tf_op jit(solution)/shard_map/ppermute | solution.py:26
  103.6 18.5 %collective-permute-start.14 = (bf16[256,64]{0,1:T(8,128)(2,1)S(1)}, bf16[256,64]{0,1:T(8,128)(2,1)S(1)}, u32[]{:S(2)}, u32[]{:S(2)}) collective-permute-start(bf16[256,64]{0,1:T(8,128)(2,1)S(1)} %collective-permute-done.10), channel_id=1, source_target_pairs={{0,4},{4,8},{8,12},{12,16},{16,20},{20,24},{24,28},{28,32},{32,36}... | collective-permute-start | bytes 98312 | tf_op jit(solution)/shard_map/ppermute | solution.py:26
  107.7 14.8 %collective-permute-start.15 = (bf16[256,32]{1,0:T(8,128)(2,1)S(1)}, bf16[256,32]{1,0:T(8,128)(2,1)S(1)}, u32[]{:S(2)}, u32[]{:S(2)}) collective-permute-start(bf16[256,32]{1,0:T(8,128)(2,1)S(1)} %collective-permute-done.11), channel_id=1, source_target_pairs={{0,4},{4,8},{8,12},{12,16},{16,20},{20,24},{24,28},{28,32},{32,36}... | collective-permute-start | bytes 49160 | tf_op jit(solution)/shard_map/ppermute | solution.py:26
  111.2 13.3 %collective-permute-start.13 = (bf16[256,32]{1,0:T(8,128)(2,1)S(1)}, bf16[256,32]{1,0:T(8,128)(2,1)S(1)}, u32[]{:S(2)}, u32[]{:S(2)}) collective-permute-start(bf16[256,32]{1,0:T(8,128)(2,1)S(1)} %collective-permute-done.9), channel_id=1, source_target_pairs={{0,508},{4,0},{8,4},{12,8},{16,12},{20,16},{24,20},{28,24},{32,28}... | collective-permute-start | bytes 49160 | tf_op jit(solution)/shard_map/ppermute | solution.py:26
where the time goes:
time: 139 us; the launch traced here: 138 us
  starting transfers between devices  82.5 us (59%)
  blocking collectives  23.4 us (17%)
  matrix products  19.2 us (14%)
  between operations  6.92 us (5%)
  local copies, waits for them, and re-layouts  5.4 us (4%)
    ppermute x16, starting transfers between devices, passed_along(): return lax.ppermute(value, axis, pairs)  78.8 us
    all_gather x1, blocking collectives, body(): own_full = lax.all_gather(features, 'feat', axis=1, tiled=True)  12.3 us
    all_to_all x1, blocking collectives, sent_and_summed(): lax.all_to_all(tiles, axis, split_axis=0, concat_axis=0, tiled=True)  11.1 us
    dot_general x9, matrix products, tile_terms(): second = jnp.dot(deriv, panel_probes, preferred_element_type=jnp.float32)  8.17 us
    dot_general x9, matrix products, tile_terms(): first = jnp.dot(kern, panel_probes, preferred_element_type=jnp.float32)  7.21 us
    dot_general x9, matrix products, tile_terms(): lax.dot_general(own_full, panel_full, (((1,), (1,)), ((), ())), preferred...  3.86 us
    all_to_all x1, starting transfers between devices, sent_to_all(): return lax.all_to_all(copies, axis, split_axis=0, concat_axis=0, tiled=True)  3.69 us
    gather x1, local copies, waits for them, and re-layouts, body(): ordered_all = jnp.take(all_probes, order[0], axis=0)  3.21 us
  transfers between devices with their start and end apart: 17, of which 0 were waited for; matrix products, arithmetic and copies ran while one was open for 16% of the time, Pallas kernels for 0%

commit v1 on v0

--- a/solution.py
+++ b/solution.py
@@ -46,7 +46,8 @@
 
 
 def body(features, probes, theta, block_mask, order):
-    own_full = lax.all_gather(features, "feat", axis=1, tiled=True)
+    sent = jnp.stack([features] * lax.axis_size("feat"))
+    own_full = jnp.concatenate(lax.all_to_all(sent, "feat", 0, 0), axis=1)
     scale = jnp.exp(-2.0 * theta[0])
     own_sq = jnp.sum(own_full.astype(jnp.float32) ** 2, axis=1)
     rows_here = probes.shape[0]

time: 139 us -> 144 us (1.036)
  blocking collectives: 23.4 us -> 12.6 us
  starting transfers between devices: 82.5 us -> 91.7 us
  waiting for transfers between devices: 0.04 us -> 7.53 us
  matrix products: 19.2 us -> 17.1 us
    all_gather x1 -> x0, blocking collectives: 12.3 us -> none  [body(): own_full = lax.all_gather(features, 'feat', axis=1, tiled=True)]
    all_to_all x1, starting transfers between devices: 3.69 us -> 10.2 us  [sent_to_all(): return lax.all_to_all(copies, axis, split_axis=0, concat_axis=0, tiled=True)]
    all_to_all x0 -> x1, starting transfers between devices: none -> 4.57 us  [body(): own_full = jnp.concatenate(lax.all_to_all(sent, 'feat', 0, 0), axis=1)]
    ppermute x16, waiting for transfers between devices: 0.04 us -> 4.39 us  [passed_along(): return lax.ppermute(value, axis, pairs)]
    all_to_all x1, waiting for transfers between devices: 0.01 us -> 3.14 us  [sent_to_all(): return lax.all_to_all(copies, axis, split_axis=0, concat_axis=0, tiled=True)]
    ppermute x16, starting transfers between devices: 78.8 us -> 76.9 us  [passed_along(): return lax.ppermute(value, axis, pairs)]
    all_to_all x1, blocking collectives: 11.1 us -> 12.6 us  [sent_and_summed(): lax.all_to_all(tiles, axis, split_axis=0, concat_axis=0, tiled=True)]
  transfers between devices with their start and end apart: 17 -> 18, of which waited for: 0 -> 2; matrix products, arithmetic and copies ran while one was open for 16% -> 12% of each run, Pallas kernels for 0% -> 0%
where the time goes in v1:
time: 144 us; the launch traced here: 143 us
  starting transfers between devices  91.7 us (64%)
  matrix products  17.1 us (12%)
  blocking collectives  12.6 us (9%)
  waiting for transfers between devices  7.53 us (5%)
  between operations  6.85 us (5%)
  local copies, waits for them, and re-layouts  6.75 us (5%)
    ppermute x16, starting transfers between devices, passed_along(): return lax.ppermute(value, axis, pairs)  76.9 us
    all_to_all x1, blocking collectives, sent_and_summed(): lax.all_to_all(tiles, axis, split_axis=0, concat_axis=0, tiled=True)  12.6 us
    all_to_all x1, starting transfers between devices, sent_to_all(): return lax.all_to_all(copies, axis, split_axis=0, concat_axis=0, tiled=True)  10.2 us
    dot_general x9, matrix products, tile_terms(): first = jnp.dot(kern, panel_probes, preferred_element_type=jnp.float32)  7.25 us
    dot_general x9, matrix products, tile_terms(): second = jnp.dot(deriv, panel_probes, preferred_element_type=jnp.float32)  6.97 us
    all_to_all x1, starting transfers between devices, body(): own_full = jnp.concatenate(lax.all_to_all(sent, 'feat', 0, 0), axis=1)  4.57 us
    ppermute x16, waiting for transfers between devices, passed_along(): return lax.ppermute(value, axis, pairs)  4.39 us
    gather x1, local copies, waits for them, and re-layouts, body(): ordered_all = jnp.take(all_probes, order[0], axis=0)  3.21 us
  transfers between devices with their start and end apart: 18, of which 2 were waited for; matrix products, arithmetic and copies ran while one was open for 12% of the time, Pallas kernels for 0%

profile of v1, /device:TPU:1, one launch (start us, length us, event | category | flops | bytes accessed | tf_op | source)
XLA Modules:
  0.0 142.9 jit_solution(7718021502665522646)
XLA Ops:
  0.6 1.3 broadcast_in_dim.13
  2.0 10.2 %all-to-all-start.1 = ((bf16[4,1024,8]{1,2,0:T(8,128)(2,1)}), bf16[4,1024,8]{1,2,0:T(8,128)(2,1)S(1)}, u32[]{:S(2)}, u32[]{:S(2)}) async-start(bf16[4,1024,8]{1,2,0:T(8,128)(2,1)} %broadcast_in_dim.13), calls=%async_computation.1 | async-start | bytes 131072 | tf_op jit(solution)/shard_map/all_to_all | solution.py:9
  12.2 0.1 dynamic-slice
  12.3 3.1 %all-to-all-done.1 = bf16[4,1024,8]{1,2,0:T(8,128)(2,1)S(1)} async-done(((bf16[4,1024,8]{1,2,0:T(8,128)(2,1)}), bf16[4,1024,8]{1,2,0:T(8,128)(2,1)S(1)}, u32[]{:S(2)}, u32[]{:S(2)}) %all-to-all-start.1) | async-done | bytes 65568 | tf_op jit(solution)/shard_map/all_to_all | solution.py:9
  15.5 0.2 copy.9
  15.6 3.2 %gather_fusion = bf16[1024,32]{1,0:T(8,128)(2,1)S(1)} fusion(bf16[1024,32]{1,0:T(8,128)(2,1)S(1)} %copy.9, s32[1024]{0:T(1024)S(1)} %broadcast_clamp_fusion), kind=kCustom, calls=%fused_computation | custom fusion | bytes 135168 | tf_op jit(solution)/shard_map/jit(_take)/gather | solution.py:73
  18.8 0.0 copy-start
  18.9 0.1 dynamic-slice_select_fusion
  19.0 1.9 %collective-permute-start.3 = (bf16[256,32]{1,0:T(8,128)(2,1)S(1)}, bf16[256,32]{1,0:T(8,128)(2,1)S(1)}, u32[]{:S(2)}, u32[]{:S(2)}) collective-permute-start(bf16[256,32]{1,0:T(8,128)(2,1)S(1)} %dynamic-slice_select_fusion), channel_id=1, source_target_pairs={{0,4},{4,8},{8,12},{12,16},{16,20},{20,24},{24,28},{28,32},{32,36}... | collective-permute-start | bytes 49160 | tf_op jit(solution)/shard_map/ppermute | solution.py:26
  20.9 10.7 %collective-permute-start.1 = (bf16[256,32]{1,0:T(8,128)(2,1)S(1)}, bf16[256,32]{1,0:T(8,128)(2,1)S(1)}, u32[]{:S(2)}, u32[]{:S(2)}) collective-permute-start(bf16[256,32]{1,0:T(8,128)(2,1)S(1)} %dynamic-slice_select_fusion), channel_id=1, source_target_pairs={{0,508},{4,0},{8,4},{12,8},{16,12},{20,16},{24,20},{28,24},{32,28}... | collective-permute-start | bytes 49160 | tf_op jit(solution)/shard_map/ppermute | solution.py:26
  31.6 0.6 stack.2
  32.2 4.6 %all-to-all-start = ((bf16[4,1024,16]{1,2,0:T(8,128)(2,1)}), bf16[4,1024,16]{1,2,0:T(8,128)(2,1)S(1)}, u32[]{:S(2)}, u32[]{:S(2)}) async-start(bf16[4,1024,16]{1,2,0:T(8,128)(2,1)} %stack.2), calls=%async_computation | async-start | bytes 262144 | tf_op jit(solution)/shard_map/all_to_all | solution.py:50
  36.8 0.0 collective-permute-done.3
  36.8 1.9 %collective-permute-start.7 = (bf16[256,32]{1,0:T(8,128)(2,1)S(1)}, bf16[256,32]{1,0:T(8,128)(2,1)S(1)}, u32[]{:S(2)}, u32[]{:S(2)}) collective-permute-start(bf16[256,32]{1,0:T(8,128)(2,1)S(1)} %collective-permute-done.3), channel_id=1, source_target_pairs={{0,4},{4,8},{8,12},{12,16},{16,20},{20,24},{24,28},{28,32},{32,36}... | collective-permute-start | bytes 49160 | tf_op jit(solution)/shard_map/ppermute | solution.py:26
  38.7 9.1 %collective-permute-start.5 = (bf16[256,32]{1,0:T(8,128)(2,1)S(1)}, bf16[256,32]{1,0:T(8,128)(2,1)S(1)}, u32[]{:S(2)}, u32[]{:S(2)}) collective-permute-start(bf16[256,32]{1,0:T(8,128)(2,1)S(1)} %collective-permute-done.1), channel_id=1, source_target_pairs={{0,508},{4,0},{8,4},{12,8},{16,12},{20,16},{24,20},{28,24},{32,28}... | collective-permute-start | bytes 49160 | tf_op jit(solution)/shard_map/ppermute | solution.py:26
  47.8 0.7 fusion.85
  54.2 0.0 collective-permute-done.7
  54.2 1.9 %collective-permute-start.11 = (bf16[256,32]{1,0:T(8,128)(2,1)S(1)}, bf16[256,32]{1,0:T(8,128)(2,1)S(1)}, u32[]{:S(2)}, u32[]{:S(2)}) collective-permute-start(bf16[256,32]{1,0:T(8,128)(2,1)S(1)} %collective-permute-done.7), channel_id=1, source_target_pairs={{0,4},{4,8},{8,12},{12,16},{16,20},{20,24},{24,28},{28,32},{32,36}... | collective-permute-start | bytes 49160 | tf_op jit(solution)/shard_map/ppermute | solution.py:26
  56.1 9.1 %collective-permute-start.9 = (bf16[256,32]{1,0:T(8,128)(2,1)S(1)}, bf16[256,32]{1,0:T(8,128)(2,1)S(1)}, u32[]{:S(2)}, u32[]{:S(2)}) collective-permute-start(bf16[256,32]{1,0:T(8,128)(2,1)S(1)} %collective-permute-done.5), channel_id=1, source_target_pairs={{0,508},{4,0},{8,4},{12,8},{16,12},{20,16},{24,20},{28,24},{32,28}... | collective-permute-start | bytes 49160 | tf_op jit(solution)/shard_map/ppermute | solution.py:26
  65.3 1.9 %collective-permute-start = (bf16[256,64]{0,1:T(8,128)(2,1)S(1)}, bf16[256,64]{0,1:T(8,128)(2,1)S(1)}, u32[]{:S(2)}, u32[]{:S(2)}) collective-permute-start(bf16[256,64]{0,1:T(8,128)(2,1)S(1)} %get-tuple-element.3), channel_id=1, source_target_pairs={{0,508},{4,0},{8,4},{12,8},{16,12},{20,16},{24,20},{28,24},{32,28}... | collective-permute-start | bytes 98312 | tf_op jit(solution)/shard_map/ppermute | solution.py:26
  67.2 3.4 %collective-permute-start.2 = (bf16[256,64]{0,1:T(8,128)(2,1)S(1)}, bf16[256,64]{0,1:T(8,128)(2,1)S(1)}, u32[]{:S(2)}, u32[]{:S(2)}) collective-permute-start(bf16[256,64]{0,1:T(8,128)(2,1)S(1)} %get-tuple-element.3), channel_id=1, source_target_pairs={{0,4},{4,8},{8,12},{12,16},{16,20},{20,24},{24,28},{28,32},{32,36}... | collective-permute-start | bytes 98312 | tf_op jit(solution)/shard_map/ppermute | solution.py:26
  70.6 0.3 fusion.11
  71.0 0.6 fusion.28
  71.6 0.6 fusion.29
  72.2 0.0 collective-permute-done.11
  72.2 1.9 %collective-permute-start.15 = (bf16[256,32]{1,0:T(8,128)(2,1)S(1)}, bf16[256,32]{1,0:T(8,128)(2,1)S(1)}, u32[]{:S(2)}, u32[]{:S(2)}) collective-permute-start(bf16[256,32]{1,0:T(8,128)(2,1)S(1)} %collective-permute-done.11), channel_id=1, source_target_pairs={{0,4},{4,8},{8,12},{12,16},{16,20},{20,24},{24,28},{28,32},{32,36}... | collective-permute-start | bytes 49160 | tf_op jit(solution)/shard_map/ppermute | solution.py:26
  74.1 0.0 collective-permute-done.9
  74.1 9.1 %collective-permute-start.13 = (bf16[256,32]{1,0:T(8,128)(2,1)S(1)}, bf16[256,32]{1,0:T(8,128)(2,1)S(1)}, u32[]{:S(2)}, u32[]{:S(2)}) collective-permute-start(bf16[256,32]{1,0:T(8,128)(2,1)S(1)} %collective-permute-done.9), channel_id=1, source_target_pairs={{0,508},{4,0},{8,4},{12,8},{16,12},{20,16},{24,20},{28,24},{32,28}... | collective-permute-start | bytes 49160 | tf_op jit(solution)/shard_map/ppermute | solution.py:26
  83.2 0.0 collective-permute-done
  83.3 1.9 %collective-permute-start.4 = (bf16[256,64]{0,1:T(8,128)(2,1)S(1)}, bf16[256,64]{0,1:T(8,128)(2,1)S(1)}, u32[]{:S(2)}, u32[]{:S(2)}) collective-permute-start(bf16[256,64]{0,1:T(8,128)(2,1)S(1)} %collective-permute-done), channel_id=1, source_target_pairs={{0,508},{4,0},{8,4},{12,8},{16,12},{20,16},{24,20},{28,24},{32,28}... | collective-permute-start | bytes 98312 | tf_op jit(solution)/shard_map/ppermute | solution.py:26
  85.2 3.4 %collective-permute-start.6 = (bf16[256,64]{0,1:T(8,128)(2,1)S(1)}, bf16[256,64]{0,1:T(8,128)(2,1)S(1)}, u32[]{:S(2)}, u32[]{:S(2)}) collective-permute-start(bf16[256,64]{0,1:T(8,128)(2,1)S(1)} %collective-permute-done.2), channel_id=1, source_target_pairs={{0,4},{4,8},{8,12},{12,16},{16,20},{20,24},{24,28},{28,32},{32,36}... | collective-permute-start | bytes 98312 | tf_op jit(solution)/shard_map/ppermute | solution.py:26
  88.6 0.3 fusion.6
  88.9 0.3 fusion.7
  89.3 0.8 fusion.19
  90.1 0.8 fusion.27
  90.9 0.8 fusion.26
  91.7 0.8 fusion.18
  92.5 0.0 collective-permute-done.4
  92.6 7.6 %collective-permute-start.8 = (bf16[256,64]{0,1:T(8,128)(2,1)S(1)}, bf16[256,64]{0,1:T(8,128)(2,1)S(1)}, u32[]{:S(2)}, u32[]{:S(2)}) collective-permute-start(bf16[256,64]{0,1:T(8,128)(2,1)S(1)} %collective-permute-done.4), channel_id=1, source_target_pairs={{0,508},{4,0},{8,4},{12,8},{16,12},{20,16},{24,20},{28,24},{32,28}... | collective-permute-start | bytes 98312 | tf_op jit(solution)/shard_map/ppermute | solution.py:26
  100.2 0.0 collective-permute-done.6
  100.3 1.9 %collective-permute-start.10 = (bf16[256,64]{0,1:T(8,128)(2,1)S(1)}, bf16[256,64]{0,1:T(8,128)(2,1)S(1)}, u32[]{:S(2)}, u32[]{:S(2)}) collective-permute-start(bf16[256,64]{0,1:T(8,128)(2,1)S(1)} %collective-permute-done.6), channel_id=1, source_target_pairs={{0,4},{4,8},{8,12},{12,16},{16,20},{20,24},{24,28},{28,32},{32,36}... | collective-permute-start | bytes 98312 | tf_op jit(solution)/shard_map/ppermute | solution.py:26
  102.2 0.3 fusion.4
  102.5 0.8 convolution_multiply_fusion.13
  103.3 0.8 convolution_multiply_fusion.21
  104.2 0.3 fusion.5
  104.5 0.8 fusion.17
  105.3 0.8 fusion.25
  106.2 9.1 %collective-permute-start.12 = (bf16[256,64]{0,1:T(8,128)(2,1)S(1)}, bf16[256,64]{0,1:T(8,128)(2,1)S(1)}, u32[]{:S(2)}, u32[]{:S(2)}) collective-permute-start(bf16[256,64]{0,1:T(8,128)(2,1)S(1)} %collective-permute-done.8), channel_id=1, source_target_pairs={{0,508},{4,0},{8,4},{12,8},{16,12},{20,16},{24,20},{28,24},{32,28}... | collective-permute-start | bytes 98312 | tf_op jit(solution)/shard_map/ppermute | solution.py:26
  115.3 2.1 %collective-permute-start.14 = (bf16[256,64]{0,1:T(8,128)(2,1)S(1)}, bf16[256,64]{0,1:T(8,128)(2,1)S(1)}, u32[]{:S(2)}, u32[]{:S(2)}) collective-permute-start(bf16[256,64]{0,1:T(8,128)(2,1)S(1)} %collective-permute-done.10), channel_id=1, source_target_pairs={{0,4},{4,8},{8,12},{12,16},{16,20},{20,24},{24,28},{28,32},{32,36}... | collective-permute-start | bytes 98312 | tf_op jit(solution)/shard_map/ppermute | solution.py:26
  117.4 0.3 fusion.2
  117.7 0.8 convolution_multiply_fusion.11
  118.5 0.8 convolution_multiply_fusion.19
  119.4 0.3 fusion.3
  119.7 0.8 fusion.23
  120.5 0.8 fusion.15
  121.3 4.3 %collective-permute-done.14 = bf16[256,64]{0,1:T(8,128)(2,1)S(1)} collective-permute-done((bf16[256,64]{0,1:T(8,128)(2,1)S(1)}, bf16[256,64]{0,1:T(8,128)(2,1)S(1)}, u32[]{:S(2)}, u32[]{:S(2)}) %collective-permute-start.14) | collective-permute-done | bytes 32800 | tf_op jit(solution)/shard_map/ppermute | solution.py:26
  125.7 0.3 fusion
  126.0 0.8 convolution_multiply_fusion.9
  126.8 0.8 convolution_multiply_fusion.17
  127.7 0.3 fusion.1
  128.0 0.8 fusion.13
  128.8 0.8 fusion.21
  129.7 12.6 %all_to_all.15 = f32[4,2048,8]{1,2,0:T(8,128)S(1)} all-to-all(f32[4,2048,8]{1,2,0:T(8,128)S(1)} %maximum_bitcast_fusion), channel_id=1, replica_groups=mesh['rows'=128,'feat'=4] {'feat'}, dimensions={0} | all-to-all | bytes 524288 | tf_op jit(solution)/shard_map/all_to_all | solution.py:37
  142.3 0.6 fusion.84
  (29 shorter events, 0.4 us)
Async XLA Ops:
  2.0 10.2 %copy-start.2 = (s32[1,1024]{1,0:T(1,128)S(1)}, s32[1,1024]{1,0:T(1,128)}, u32[]{:S(2)}) copy-start(s32[1,1024]{1,0:T(1,128)} %param.9) | copy-start | bytes 12292
  2.0 13.5 %all-to-all-start.1 = ((bf16[4,1024,8]{1,2,0:T(8,128)(2,1)}), bf16[4,1024,8]{1,2,0:T(8,128)(2,1)S(1)}, u32[]{:S(2)}, u32[]{:S(2)}) async-start(bf16[4,1024,8]{1,2,0:T(8,128)(2,1)} %broadcast_in_dim.13), calls=%async_computation.1 | async-start | bytes 131072 | tf_op jit(solution)/shard_map/all_to_all | solution.py:9
  18.8 12.7 %copy-start = (bf16[1024,16]{0,1:T(8,128)(2,1)S(1)}, bf16[1024,16]{0,1:T(8,128)(2,1)}, u32[]{:S(2)}) copy-start(bf16[1024,16]{0,1:T(8,128)(2,1)} %param.5) | copy-start | bytes 98308
  19.0 17.9 %collective-permute-start.3 = (bf16[256,32]{1,0:T(8,128)(2,1)S(1)}, bf16[256,32]{1,0:T(8,128)(2,1)S(1)}, u32[]{:S(2)}, u32[]{:S(2)}) collective-permute-start(bf16[256,32]{1,0:T(8,128)(2,1)S(1)} %dynamic-slice_select_fusion), channel_id=1, source_target_pairs={{0,4},{4,8},{8,12},{12,16},{16,20},{20,24},{24,28},{28,32},{32,36}... | collective-permute-start | bytes 49160 | tf_op jit(solution)/shard_map/ppermute | solution.py:26
  20.9 17.8 %collective-permute-start.1 = (bf16[256,32]{1,0:T(8,128)(2,1)S(1)}, bf16[256,32]{1,0:T(8,128)(2,1)S(1)}, u32[]{:S(2)}, u32[]{:S(2)}) collective-permute-start(bf16[256,32]{1,0:T(8,128)(2,1)S(1)} %dynamic-slice_select_fusion), channel_id=1, source_target_pairs={{0,508},{4,0},{8,4},{12,8},{16,12},{20,16},{24,20},{28,24},{32,28}... | collective-permute-start | bytes 49160 | tf_op jit(solution)/shard_map/ppermute | solution.py:26
  32.2 15.6 %copy-start.1 = (s32[1,9]{1,0:T(1,128)S(1)}, s32[1,9]{1,0:T(1,128)}, u32[]{:S(2)}) copy-start(s32[1,9]{1,0:T(1,128)} %param.8) | copy-start | bytes 112
  32.2 33.0 %all-to-all-start = ((bf16[4,1024,16]{1,2,0:T(8,128)(2,1)}), bf16[4,1024,16]{1,2,0:T(8,128)(2,1)S(1)}, u32[]{:S(2)}, u32[]{:S(2)}) async-start(bf16[4,1024,16]{1,2,0:T(8,128)(2,1)} %stack.2), calls=%async_computation | async-start | bytes 262144 | tf_op jit(solution)/shard_map/all_to_all | solution.py:50
  36.8 17.4 %collective-permute-start.7 = (bf16[256,32]{1,0:T(8,128)(2,1)S(1)}, bf16[256,32]{1,0:T(8,128)(2,1)S(1)}, u32[]{:S(2)}, u32[]{:S(2)}) collective-permute-start(bf16[256,32]{1,0:T(8,128)(2,1)S(1)} %collective-permute-done.3), channel_id=1, source_target_pairs={{0,4},{4,8},{8,12},{12,16},{16,20},{20,24},{24,28},{28,32},{32,36}... | collective-permute-start | bytes 49160 | tf_op jit(solution)/shard_map/ppermute | solution.py:26
  38.7 17.4 %collective-permute-start.5 = (bf16[256,32]{1,0:T(8,128)(2,1)S(1)}, bf16[256,32]{1,0:T(8,128)(2,1)S(1)}, u32[]{:S(2)}, u32[]{:S(2)}) collective-permute-start(bf16[256,32]{1,0:T(8,128)(2,1)S(1)} %collective-permute-done.1), channel_id=1, source_target_pairs={{0,508},{4,0},{8,4},{12,8},{16,12},{20,16},{24,20},{28,24},{32,28}... | collective-permute-start | bytes 49160 | tf_op jit(solution)/shard_map/ppermute | solution.py:26
  54.2 18.0 %collective-permute-start.11 = (bf16[256,32]{1,0:T(8,128)(2,1)S(1)}, bf16[256,32]{1,0:T(8,128)(2,1)S(1)}, u32[]{:S(2)}, u32[]{:S(2)}) collective-permute-start(bf16[256,32]{1,0:T(8,128)(2,1)S(1)} %collective-permute-done.7), channel_id=1, source_target_pairs={{0,4},{4,8},{8,12},{12,16},{16,20},{20,24},{24,28},{28,32},{32,36}... | collective-permute-start | bytes 49160 | tf_op jit(solution)/shard_map/ppermute | solution.py:26
  56.1 18.0 %collective-permute-start.9 = (bf16[256,32]{1,0:T(8,128)(2,1)S(1)}, bf16[256,32]{1,0:T(8,128)(2,1)S(1)}, u32[]{:S(2)}, u32[]{:S(2)}) collective-permute-start(bf16[256,32]{1,0:T(8,128)(2,1)S(1)} %collective-permute-done.5), channel_id=1, source_target_pairs={{0,508},{4,0},{8,4},{12,8},{16,12},{20,16},{24,20},{28,24},{32,28}... | collective-permute-start | bytes 49160 | tf_op jit(solution)/shard_map/ppermute | solution.py:26
  65.3 18.0 %collective-permute-start = (bf16[256,64]{0,1:T(8,128)(2,1)S(1)}, bf16[256,64]{0,1:T(8,128)(2,1)S(1)}, u32[]{:S(2)}, u32[]{:S(2)}) collective-permute-start(bf16[256,64]{0,1:T(8,128)(2,1)S(1)} %get-tuple-element.3), channel_id=1, source_target_pairs={{0,508},{4,0},{8,4},{12,8},{16,12},{20,16},{24,20},{28,24},{32,28}... | collective-permute-start | bytes 98312 | tf_op jit(solution)/shard_map/ppermute | solution.py:26
  67.2 18.0 %collective-permute-start.2 = (bf16[256,64]{0,1:T(8,128)(2,1)S(1)}, bf16[256,64]{0,1:T(8,128)(2,1)S(1)}, u32[]{:S(2)}, u32[]{:S(2)}) collective-permute-start(bf16[256,64]{0,1:T(8,128)(2,1)S(1)} %get-tuple-element.3), channel_id=1, source_target_pairs={{0,4},{4,8},{8,12},{12,16},{16,20},{20,24},{24,28},{28,32},{32,36}... | collective-permute-start | bytes 98312 | tf_op jit(solution)/shard_map/ppermute | solution.py:26
  72.2 53.8 %collective-permute-start.15 = (bf16[256,32]{1,0:T(8,128)(2,1)S(1)}, bf16[256,32]{1,0:T(8,128)(2,1)S(1)}, u32[]{:S(2)}, u32[]{:S(2)}) collective-permute-start(bf16[256,32]{1,0:T(8,128)(2,1)S(1)} %collective-permute-done.11), channel_id=1, source_target_pairs={{0,4},{4,8},{8,12},{12,16},{16,20},{20,24},{24,28},{28,32},{32,36}... | collective-permute-start | bytes 49160 | tf_op jit(solution)/shard_map/ppermute | solution.py:26
  74.1 53.9 %collective-permute-start.13 = (bf16[256,32]{1,0:T(8,128)(2,1)S(1)}, bf16[256,32]{1,0:T(8,128)(2,1)S(1)}, u32[]{:S(2)}, u32[]{:S(2)}) collective-permute-start(bf16[256,32]{1,0:T(8,128)(2,1)S(1)} %collective-permute-done.9), channel_id=1, source_target_pairs={{0,508},{4,0},{8,4},{12,8},{16,12},{20,16},{24,20},{28,24},{32,28}... | collective-permute-start | bytes 49160 | tf_op jit(solution)/shard_map/ppermute | solution.py:26
  83.3 9.3 %collective-permute-start.4 = (bf16[256,64]{0,1:T(8,128)(2,1)S(1)}, bf16[256,64]{0,1:T(8,128)(2,1)S(1)}, u32[]{:S(2)}, u32[]{:S(2)}) collective-permute-start(bf16[256,64]{0,1:T(8,128)(2,1)S(1)} %collective-permute-done), channel_id=1, source_target_pairs={{0,508},{4,0},{8,4},{12,8},{16,12},{20,16},{24,20},{28,24},{32,28}... | collective-permute-start | bytes 98312 | tf_op jit(solution)/shard_map/ppermute | solution.py:26
  85.2 15.0 %collective-permute-start.6 = (bf16[256,64]{0,1:T(8,128)(2,1)S(1)}, bf16[256,64]{0,1:T(8,128)(2,1)S(1)}, u32[]{:S(2)}, u32[]{:S(2)}) collective-permute-start(bf16[256,64]{0,1:T(8,128)(2,1)S(1)} %collective-permute-done.2), channel_id=1, source_target_pairs={{0,4},{4,8},{8,12},{12,16},{16,20},{20,24},{24,28},{28,32},{32,36}... | collective-permute-start | bytes 98312 | tf_op jit(solution)/shard_map/ppermute | solution.py:26
  92.6 13.5 %collective-permute-start.8 = (bf16[256,64]{0,1:T(8,128)(2,1)S(1)}, bf16[256,64]{0,1:T(8,128)(2,1)S(1)}, u32[]{:S(2)}, u32[]{:S(2)}) collective-permute-start(bf16[256,64]{0,1:T(8,128)(2,1)S(1)} %collective-permute-done.4), channel_id=1, source_target_pairs={{0,508},{4,0},{8,4},{12,8},{16,12},{20,16},{24,20},{28,24},{32,28}... | collective-permute-start | bytes 98312 | tf_op jit(solution)/shard_map/ppermute | solution.py:26
  100.3 15.0 %collective-permute-start.10 = (bf16[256,64]{0,1:T(8,128)(2,1)S(1)}, bf16[256,64]{0,1:T(8,128)(2,1)S(1)}, u32[]{:S(2)}, u32[]{:S(2)}) collective-permute-start(bf16[256,64]{0,1:T(8,128)(2,1)S(1)} %collective-permute-done.6), channel_id=1, source_target_pairs={{0,4},{4,8},{8,12},{12,16},{16,20},{20,24},{24,28},{28,32},{32,36}... | collective-permute-start | bytes 98312 | tf_op jit(solution)/shard_map/ppermute | solution.py:26
  106.2 21.5 %collective-permute-start.12 = (bf16[256,64]{0,1:T(8,128)(2,1)S(1)}, bf16[256,64]{0,1:T(8,128)(2,1)S(1)}, u32[]{:S(2)}, u32[]{:S(2)}) collective-permute-start(bf16[256,64]{0,1:T(8,128)(2,1)S(1)} %collective-permute-done.8), channel_id=1, source_target_pairs={{0,508},{4,0},{8,4},{12,8},{16,12},{20,16},{24,20},{28,24},{32,28}... | collective-permute-start | bytes 98312 | tf_op jit(solution)/shard_map/ppermute | solution.py:26
  115.3 10.4 %collective-permute-start.14 = (bf16[256,64]{0,1:T(8,128)(2,1)S(1)}, bf16[256,64]{0,1:T(8,128)(2,1)S(1)}, u32[]{:S(2)}, u32[]{:S(2)}) collective-permute-start(bf16[256,64]{0,1:T(8,128)(2,1)S(1)} %collective-permute-done.10), channel_id=1, source_target_pairs={{0,4},{4,8},{8,12},{12,16},{16,20},{20,24},{24,28},{28,32},{32,36}... | collective-permute-start | bytes 98312 | tf_op jit(solution)/shard_map/ppermute | solution.py:26
